TPU v7x, 256 devices: a whole 4x4x8 slice. The times are simulated.
256 devices in a mesh: expert: 8 (over y_lo, x), rep: 32 (over z, y_hi, core).
Axes of the slice: x: 4, y: 4 (y_hi: 2, y_lo: 2; y = y_hi * 2 + y_lo), z: 8, core: 2. Of those that a mesh axis runs over, the one named last changes fastest.
Arguments:
- route_ids: int32 [2048, 2], P(('expert', 'rep')), may hold values from 0 to 7, all different within a row; in each aligned block of 8 rows (0 to 7, 8 to 15, ...) at most 4 rows name the same one
- route_weight: float32 [2048, 2], P(('expert', 'rep')), may hold values from 0.2 to 0.8
- input_float: bfloat16 [2048, 4096], P(('expert', 'rep')), may hold values from -6 to 6
- input_quant: bfloat16 [2048, 4096], P(('expert', 'rep')), may hold values from -6 to 6
- keep_mask: int32 [2048, 4096], P(('expert', 'rep')), may hold values 0 or 1
- grad_mixed: bfloat16 [2048, 4096], P(('expert', 'rep')), may hold values from -192 to 192
- gate_weight: bfloat16 [8, 4096, 7168], P('expert', None, 'rep'), may hold values from -0.09375 to 0.09375
- up_weight: bfloat16 [8, 4096, 7168], P('expert', None, 'rep'), may hold values from -0.09375 to 0.09375
- down_base: bfloat16 [8, 7168, 4096], P('expert', 'rep'), may hold values from -0.0625 to 0.0625
- down_round: bfloat16 [8, 7168, 4096], P('expert', 'rep'), may hold values from -8 to 8
- down_step: float32 [8, 4096], P('expert'), may hold values from 0.004 to 0.04
Outputs:
- mixed: bfloat16 [2048, 4096], P(('expert', 'rep'))
- round_grad: float32 [8, 7168, 4096], P('expert', 'rep')
Inputs may be any that keep to these rules, and one draw needn't show every extreme that they name: `route_ids`: within the 8 tokens of one device, each expert is named by at most 4 pairs; the two experts of a token differ.
All inputs are finite; a program needn't handle non-finite values. No bound on the sum of `keep_mask` on one device may be relied on, other than what follows from the above.
Results may differ from a plain program's by a relative error of at most 0.0065.
Values may be sent and summed in bfloat16 or wider, within the bound.
No kernel may reach another device: no remote copies, remote signals or barrier semaphores. Data moves between devices by JAX's collectives and lax.ppermute only.
A program may use at most 128 MiB of HBM per device.

v0:
```python
import jax
import jax.numpy as jnp
from jax import lax
from jax.sharding import PartitionSpec as P


def in_one_piece(arrays, axis, split_dim, concat_dim, along):
    both = jnp.concatenate(arrays, axis=along)
    filled, at, gathered = (
        lax.all_to_all(both, axis, split_axis=split_dim, concat_axis=concat_dim, tiled=True),
        0,
        [],
    )
    for a in arrays:
        gathered.append(lax.slice_in_dim(filled, at, at + a.shape[along], axis=along))
        at += a.shape[along]
    return tuple(gathered)


def sent_together(arrays, axis, dim, along):
    ends, at = ([], 0)
    for a in arrays[:-1]:
        at += a.shape[along]
        ends.append(at)
    both = jnp.concatenate(arrays, axis=along)
    return tuple(jnp.split(lax.all_gather(both, axis, axis=dim, tiled=True), ends, axis=along))


def local_slots(route_ids, experts):
    count = route_ids.shape[0]
    flat = route_ids.reshape(count * 2)
    onehot = (flat[:, None] == jnp.arange(experts, dtype=jnp.int32)[None, :]).astype(jnp.int32)
    before = jnp.cumsum(onehot, axis=0) - onehot
    return jnp.sum(before * onehot, axis=1).reshape(count, 2)


def body(
    route_ids,
    route_weight,
    input_float,
    input_quant,
    keep_mask,
    grad_mixed,
    gate_weight,
    up_weight,
    down_base,
    down_round,
    down_step,
):
    experts = lax.axis_size("expert")
    count = route_ids.shape[0]
    capacity = count // 2
    slot = local_slots(route_ids, experts)
    target = route_ids * capacity + slot
    columns = jnp.arange(experts * capacity, dtype=jnp.int32)
    first = (target[:, 0:1] == columns[None, :]).astype(jnp.float32)
    second = (target[:, 1:2] == columns[None, :]).astype(jnp.float32)
    placing = (first + second).astype(jnp.bfloat16)
    weighting = route_weight[:, 0:1] * first + route_weight[:, 1:2] * second
    x_in = jnp.where(keep_mask == 1, input_quant, input_float)
    send_rows = lax.dot_general(
        placing, x_in, (((0,), (0,)), ((), ())), preferred_element_type=jnp.float32
    ).astype(jnp.bfloat16)
    send_cot = lax.dot_general(
        weighting,
        grad_mixed.astype(jnp.float32),
        (((0,), (0,)), ((), ())),
        precision=lax.Precision.HIGHEST,
        preferred_element_type=jnp.float32,
    ).astype(jnp.bfloat16)
    own_rows, own_cot = in_one_piece((send_rows, send_cot), "expert", 0, 0, 1)
    w_gate = gate_weight[0]
    w_up = up_weight[0]
    soft = jax.nn.sigmoid(down_round[0].astype(jnp.float32))
    step_row = down_step[0][None, :]
    quant_down = (down_base[0].astype(jnp.float32) + step_row * soft).astype(jnp.bfloat16)
    all_rows, all_cot = sent_together((own_rows, own_cot), "rep", 0, 1)
    gate = jnp.dot(all_rows, w_gate, preferred_element_type=jnp.float32)
    up = jnp.dot(all_rows, w_up, preferred_element_type=jnp.float32)
    hidden = (jax.nn.silu(gate) * up).astype(jnp.bfloat16)
    grad_w = lax.dot_general(
        hidden, all_cot, (((0,), (0,)), ((), ())), preferred_element_type=jnp.float32
    )
    wide_down = lax.all_to_all(quant_down, "rep", split_axis=1, concat_axis=0, tiled=True)
    out_cols = jnp.dot(
        lax.all_gather(hidden, "rep", axis=1, tiled=True),
        wide_down,
        preferred_element_type=jnp.float32,
    )
    summed = lax.all_to_all(
        out_cols.astype(jnp.bfloat16), "rep", split_axis=0, concat_axis=1, tiled=True
    )
    returned = lax.all_to_all(summed, "expert", split_axis=0, concat_axis=0, tiled=True)
    mixed = jnp.dot(
        weighting,
        returned.astype(jnp.float32),
        precision=lax.Precision.HIGHEST,
        preferred_element_type=jnp.float32,
    ).astype(jnp.bfloat16)
    round_grad = (grad_w * step_row * soft * (1.0 - soft))[None]
    return (mixed, round_grad)


def solution(mesh):
    return jax.shard_map(
        body,
        mesh=mesh,
        in_specs=(
            P(("expert", "rep"), None),
            P(("expert", "rep"), None),
            P(("expert", "rep"), None),
            P(("expert", "rep"), None),
            P(("expert", "rep"), None),
            P(("expert", "rep"), None),
            P("expert", None, "rep"),
            P("expert", None, "rep"),
            P("expert", "rep", None),
            P("expert", "rep", None),
            P("expert", None),
        ),
        out_specs=(P(("expert", "rep"), None), P("expert", "rep", None)),
        check_vma=False,
    )
```

profile of v0, /device:TPU:1, one launch (start us, length us, event | category | flops | bytes accessed | tf_op | source)
XLA Modules:
  0.0 381.1 jit_solution(1803155560595772534)
XLA Ops:
  7.2 0.8 slice_bitcast_fusion.1
  8.1 0.8 copy.23
  9.5 1.3 convolution_convert_fusion.1
  10.8 1.3 convolution_convert_fusion
  12.3 14.9 %all_to_all.56 = bf16[8,4,8192]{2,1,0:T(4,128)(2,1)S(1)} all-to-all(bf16[8,4,8192]{2,1,0:T(4,128)(2,1)S(1)} %all_to_all.40), channel_id=1, replica_groups=mesh['expert'=8,'rep'=32] {'expert'}, dimensions={0} | all-to-all | bytes 1048576 | tf_op jit(solution)/shard_map/all_to_all | solution.py:10
  27.2 0.9 all_to_all.42
  28.2 139.6 %all-gather.3.cloned.1.call-done = bf16[1024,8192]{1,0:T(8,128)(2,1)} async-done(((bf16[32,8192]{1,0:T(8,128)(2,1)}), bf16[1024,8192]{1,0:T(8,128)(2,1)}) %all-gather.3.cloned.1.call-update) | async-done | bytes 16777232 | tf_op jit(solution)/shard_map/all_gather | solution.py:26
  167.8 6.1 %fusion.4 = f32[1024,224]{0,1:T(8,128)S(1)} fusion(bf16[1024,8192]{1,0:T(8,128)(2,1)} %all-gather.3.cloned.1.call-done, bf16[1,4096,224]{1,2,0:T(8,128)(2,1)S(1)} %copy-done), kind=kOutput, calls=%fused_computation.4 | convolution fusion | flops 1879048192 | bytes 11141120 | tf_op jit(solution)/shard_map/dot_general | solution.py:78
  174.0 2.0 copy-done.6
  176.5 3.5 fusion.28
  180.5 0.6 copy.27
  181.1 0.8 copy-done.3
  182.0 1.0 fusion.22
  182.9 0.6 copy.28
  183.6 0.9 fusion.19
  184.6 0.7 copy.25
  185.3 67.5 %all_to_all.57 = bf16[224,32,128]{2,0,1:T(8,128)(2,1)S(1)} all-to-all(bf16[224,32,128]{2,0,1:T(8,128)(2,1)S(1)} %copy.25), channel_id=1, replica_groups=mesh['expert'=8,'rep'=32] {'rep'}, dimensions={1} | all-to-all | bytes 3670016 | tf_op jit(solution)/shard_map/all_to_all | solution.py:84
  252.8 81.7 %all-gather.5.cloned.1.call-done = bf16[1024,7168]{0,1:T(8,128)(2,1)} async-done(((bf16[1024,224]{0,1:T(8,128)(2,1)}), bf16[1024,7168]{0,1:T(8,128)(2,1)}) %all-gather.5.cloned.1.call-update) | async-done | bytes 14680080 | tf_op jit(solution)/shard_map/all_gather | solution.py:86
  334.5 7.3 %convolution_convert_fusion.3 = bf16[1024,128]{1,0:T(8,128)(2,1)S(1)} fusion(bf16[1024,7168]{0,1:T(8,128)(2,1)} %all-gather.5.cloned.1.call-done, bf16[7168,128]{1,0:T(8,128)(2,1)S(1)} %bitcast.47), kind=kOutput, calls=%fused_computation.24 | convolution fusion | flops 1879179264 | bytes 16777216 | tf_op jit(solution)/shard_map/dot_general | solution.py:85
  341.9 17.4 %all_to_all.58 = bf16[32,32,128]{2,1,0:T(8,128)(2,1)S(1)} all-to-all(bf16[32,32,128]{2,1,0:T(8,128)(2,1)S(1)} %bitcast.49), channel_id=1, replica_groups=mesh['expert'=8,'rep'=32] {'rep'}, dimensions={0} | all-to-all | bytes 524288 | tf_op jit(solution)/shard_map/all_to_all | solution.py:90
  359.4 0.8 all_to_all.49
  360.2 4.8 %all-to-all-start.3 = ((bf16[8,4,4096]{2,1,0:T(4,128)(2,1)}), bf16[8,4,4096]{2,1,0:T(4,128)(2,1)S(1)}, u32[]{:S(2)}, u32[]{:S(2)}) async-start(bf16[8,4,4096]{2,1,0:T(4,128)(2,1)} %all_to_all.49), calls=%async_computation.3 | async-start | bytes 524288 | tf_op jit(solution)/shard_map/all_to_all | solution.py:93
  365.1 8.2 %fusion.15 = f32[1,224,4096]{2,1,0:T(8,128)} fusion(bf16[1024,224]{0,1:T(8,128)(2,1)S(1)} %copy-done.4, bf16[1024,8192]{1,0:T(8,128)(2,1)} %all-gather.3.cloned.1.call-done, f32[4096]{0:T(1024)S(1)} %bitcast.51, bf16[1,224,4096]{2,1,0:T(8,128)(2,1)} %param.20), kind=kOutput, calls=%fused_computation.9 | convolution fusion | flops 1886388224 | bytes 14368768 | tf_op jit(solution)/shard_map/dot_general | solution.py:81
  373.3 0.9 convolution_convert_fusion.2
  (31 shorter events, 2.2 us)
Async XLA Ops:
  7.2 160.7 %copy-start = (bf16[1,4096,224]{1,2,0:T(8,128)(2,1)S(1)}, bf16[1,4096,224]{1,2,0:T(8,128)(2,1)}, u32[]{:S(2)}) copy-start(bf16[1,4096,224]{1,2,0:T(8,128)(2,1)} %param.17) | copy-start | bytes 5505028
  7.2 160.6 %all-gather.3.cloned.1.call-start = ((), (), s32[]{:S(2)}) async-start(), calls=%async_computation.4 | async-start | bytes 17301504 | tf_op jit(solution)/shard_map/all_gather | solution.py:26
  28.2 306.3 %all-gather.5.cloned.1.call-start = ((), (), s32[]{:S(2)}) async-start(), calls=%async_computation.5 | async-start | bytes 15138816 | tf_op jit(solution)/shard_map/all_gather | solution.py:86
  167.8 8.2 %copy-start.6 = (bf16[1024,8192]{1,0:T(8,128)(2,1)S(1)}, bf16[1024,8192]{1,0:T(8,128)(2,1)}, u32[]{:S(2)}) copy-start(bf16[1024,8192]{1,0:T(8,128)(2,1)} %all-gather.3.cloned.1.call-done) | copy-start | bytes 50331652
  167.8 8.7 %copy-start.7 = (bf16[1,4096,224]{1,2,0:T(8,128)(2,1)S(1)}, bf16[1,4096,224]{1,2,0:T(8,128)(2,1)}, u32[]{:S(2)}) copy-start(bf16[1,4096,224]{1,2,0:T(8,128)(2,1)} %param.18) | copy-start | bytes 5505028
  176.5 3.6 copy-start.2
  180.5 1.5 copy-start.3
  182.9 0.7 copy-start.5
  334.5 30.5 %copy-start.4 = (bf16[1024,224]{0,1:T(8,128)(2,1)S(1)}, bf16[1024,224]{0,1:T(8,128)(2,1)}, u32[]{:S(2)}) copy-start(bf16[1024,224]{0,1:T(8,128)(2,1)} %fusion.28) | copy-start | bytes 1376260
  360.2 13.1 %all-to-all-start.3 = ((bf16[8,4,4096]{2,1,0:T(4,128)(2,1)}), bf16[8,4,4096]{2,1,0:T(4,128)(2,1)S(1)}, u32[]{:S(2)}, u32[]{:S(2)}) async-start(bf16[8,4,4096]{2,1,0:T(4,128)(2,1)} %all_to_all.49), calls=%async_computation.3 | async-start | bytes 524288 | tf_op jit(solution)/shard_map/all_to_all | solution.py:93
  365.0 9.2 %copy-start.1 = (bf16[1,4096,224]{1,2,0:T(8,128)(2,1)S(1)}, bf16[1,4096,224]{1,2,0:T(8,128)(2,1)}, u32[]{:S(2)}) copy-start(bf16[1,4096,224]{1,2,0:T(8,128)(2,1)} %param.17) | copy-start | bytes 5505028
Sparse Core Ops, SparseCore 0:
  28.3 139.4 all-gather.2
  180.2 154.3 all-gather.4
where the time goes:
time: 382 us; the launch traced here: 381 us
  waiting for transfers between devices  221 us (58%)
  blocking collectives  99.8 us (26%)
  matrix products  28.8 us (8%)
  between operations  14.2 us (4%)
  local copies, waits for them, and re-layouts  9.41 us (2%)
  starting transfers between devices  4.93 us (1%)
    all_gather x1, waiting for transfers between devices, sent_together(): lax.all_gather(both, axis, axis=dim, tiled=True)  140 us
    all_gather x1, waiting for transfers between devices, body(): lax.all_gather(hidden, 'rep', axis=1, tiled=True)  81.7 us
    all_to_all x1, blocking collectives, body(): lax.all_to_all(quant_down, 'rep', split_axis=1, concat_axis=0, tiled=True)  67.5 us
    all_to_all x1, blocking collectives, body(): lax.all_to_all(out_cols.astype(jnp.bfloat16), 'rep', split_axis=0, concat...  17.4 us
    all_to_all x1, blocking collectives, in_one_piece(): lax.all_to_all(both, axis, split_axis=split_dim, concat_axis=concat_dim,...  14.9 us
    dot_general x1, matrix products, body(): lax.dot_general(hidden, all_cot, (((0,), (0,)), ((), ())), preferred_elem...  8.21 us
  transfers between devices with their start and end apart: 3, of which 2 were waited for; matrix products, arithmetic and copies ran while one was open for 3% of the time, Pallas kernels for 0%

commit v1 on v0

--- a/solution.py
+++ b/solution.py
@@ -1,7 +1,15 @@
+import functools
 import jax
 import jax.numpy as jnp
 from jax import lax
 from jax.sharding import PartitionSpec as P
+
+
+def zone_compute(tile_in, device_axis):
+    return jnp.concatenate(lax.all_gather(tile_in, device_axis), axis=1)
+
+
+start_regions_for = functools.partial(zone_compute, device_axis="rep")
 
 
 def in_one_piece(arrays, axis, split_dim, concat_dim, along):
@@ -82,11 +90,7 @@
         hidden, all_cot, (((0,), (0,)), ((), ())), preferred_element_type=jnp.float32
     )
     wide_down = lax.all_to_all(quant_down, "rep", split_axis=1, concat_axis=0, tiled=True)
-    out_cols = jnp.dot(
-        lax.all_gather(hidden, "rep", axis=1, tiled=True),
-        wide_down,
-        preferred_element_type=jnp.float32,
-    )
+    out_cols = jnp.dot(start_regions_for(hidden), wide_down, preferred_element_type=jnp.float32)
     summed = lax.all_to_all(
         out_cols.astype(jnp.bfloat16), "rep", split_axis=0, concat_axis=1, tiled=True
     )

time: 382 us -> 399 us (1.045)
  blocking collectives: 99.8 us -> 32.3 us
  waiting for transfers between devices: 221 us -> 283 us
  local copies, waits for them, and re-layouts: 9.41 us -> 27.3 us
  starting transfers between devices: 4.93 us -> 9.63 us
    all_to_all x1 -> x0, blocking collectives: 67.5 us -> none  [body(): lax.all_to_all(quant_down, 'rep', split_axis=1, concat_axis=0, tiled=True)]
    all_gather x1, waiting for transfers between devices: 81.7 us -> 143 us  [zone_compute(): return jnp.concatenate(lax.all_gather(tile_in, device_axis), axis=1)]
    unnamed x19 -> x20, local copies, waits for them, and re-layouts: 5.48 us -> 22.1 us
    all_to_all x0 -> x1, starting transfers between devices: none -> 4.7 us  [body(): lax.all_to_all(quant_down, 'rep', split_axis=1, concat_axis=0, tiled=True)]
  transfers between devices with their start and end apart: 3 -> 4, of which waited for: 2 -> 2; matrix products, arithmetic and copies ran while one was open for 3% -> 8% of each run, Pallas kernels for 0% -> 0%
where the time goes in v1:
time: 399 us; the launch traced here: 398 us
  waiting for transfers between devices  283 us (71%)
  blocking collectives  32.3 us (8%)
  matrix products  28.9 us (7%)
  local copies, waits for them, and re-layouts  27.3 us (7%)
  between operations  14.2 us (4%)
  starting transfers between devices  9.63 us (2%)
    all_gather x1, waiting for transfers between devices, zone_compute(): return jnp.concatenate(lax.all_gather(tile_in, device_axis), axis=1)  143 us
    all_gather x1, waiting for transfers between devices, sent_together(): lax.all_gather(both, axis, axis=dim, tiled=True)  140 us
    unnamed x20, local copies, waits for them, and re-layouts  22.1 us
    all_to_all x1, blocking collectives, body(): lax.all_to_all(out_cols.astype(jnp.bfloat16), 'rep', split_axis=0, concat...  17.4 us
    all_to_all x1, blocking collectives, in_one_piece(): lax.all_to_all(both, axis, split_axis=split_dim, concat_axis=concat_dim,...  14.9 us
    dot_general x1, matrix products, body(): lax.dot_general(hidden, all_cot, (((0,), (0,)), ((), ())), preferred_elem...  8.21 us
  transfers between devices with their start and end apart: 4, of which 2 were waited for; matrix products, arithmetic and copies ran while one was open for 8% of the time, Pallas kernels for 0%

profile of v1, /device:TPU:1, one launch (start us, length us, event | category | flops | bytes accessed | tf_op | source)
XLA Modules:
  0.0 397.9 jit_solution(9273424431898968779)
XLA Ops:
  7.2 0.8 slice_bitcast_fusion.1
  8.1 0.8 copy.25
  9.5 1.3 convolution_convert_fusion.1
  10.8 1.3 convolution_convert_fusion
  12.3 14.9 %all_to_all.53 = bf16[8,4,8192]{2,1,0:T(4,128)(2,1)S(1)} all-to-all(bf16[8,4,8192]{2,1,0:T(4,128)(2,1)S(1)} %all_to_all.38), channel_id=1, replica_groups=mesh['expert'=8,'rep'=32] {'expert'}, dimensions={0} | all-to-all | bytes 1048576 | tf_op jit(solution)/shard_map/all_to_all | solution.py:18
  27.2 0.9 all_to_all.40
  28.2 139.6 %all-gather.4.cloned.1.call-done = bf16[1024,8192]{1,0:T(8,128)(2,1)} async-done(((bf16[32,8192]{1,0:T(8,128)(2,1)}), bf16[1024,8192]{1,0:T(8,128)(2,1)}) %all-gather.4.cloned.1.call-update) | async-done | bytes 16777232 | tf_op jit(solution)/shard_map/all_gather | solution.py:34
  167.8 6.1 %fusion.6 = f32[1024,224]{0,1:T(8,128)S(1)} fusion(bf16[1024,8192]{1,0:T(8,128)(2,1)} %all-gather.4.cloned.1.call-done, bf16[1,4096,224]{1,2,0:T(8,128)(2,1)S(1)} %copy-done), kind=kOutput, calls=%fused_computation.6 | convolution fusion | flops 1879048192 | bytes 11141120 | tf_op jit(solution)/shard_map/dot_general | solution.py:86
  174.0 2.0 copy-done.6
  176.5 3.5 fusion.32
  180.5 0.6 copy.31
  181.1 0.8 copy-done.3
  182.0 1.0 fusion.26
  183.7 0.9 fusion.21
  184.6 1.9 copy.27
  186.5 4.7 %all-to-all-start.1 = ((bf16[224,32,128]{2,0,1:T(8,128)(2,1)}), bf16[224,32,128]{2,0,1:T(8,128)(2,1)S(1)}, u32[]{:S(2)}, u32[]{:S(2)}) async-start(bf16[224,32,128]{2,0,1:T(8,128)(2,1)} %copy.27), calls=%async_computation.1 | async-start | bytes 3670016 | tf_op jit(solution)/shard_map/all_to_all | solution.py:92
  191.2 143.4 %all-gather.6.cloned.1.call-done = bf16[32768,224]{0,1:T(8,128)(2,1)} async-done(((bf16[1024,224]{0,1:T(8,128)(2,1)}), bf16[32768,224]{0,1:T(8,128)(2,1)}) %all-gather.6.cloned.1.call-update) | async-done | bytes 14680080 | tf_op jit(solution)/shard_map/all_gather | solution.py:9
  334.6 16.6 %copy.30 = bf16[28,8,32,1024]{3,2,1,0:T(8,128)(2,1)} copy(bf16[28,8,32,1024]{3,1,2,0:T(8,128)(2,1)} %bitcast.64) | data formatting | bytes 29360128
  351.2 7.4 %fusion.42 = bf16[1024,128]{1,0:T(8,128)(2,1)S(1)} fusion(bf16[224,32,128]{2,0,1:T(8,128)(2,1)S(1)} %all-to-all-done.1, bf16[32,1024,224]{1,0,2:T(8,128)(2,1)} %bitcast.65), kind=kOutput, calls=%fused_computation.29 | convolution fusion | flops 1879179264 | bytes 16777216 | tf_op jit(solution)/shard_map/dot_general | solution.py:93
  358.7 17.4 %all_to_all.54 = bf16[32,32,128]{2,1,0:T(8,128)(2,1)S(1)} all-to-all(bf16[32,32,128]{2,1,0:T(8,128)(2,1)S(1)} %bitcast.67), channel_id=1, replica_groups=mesh['expert'=8,'rep'=32] {'rep'}, dimensions={0} | all-to-all | bytes 524288 | tf_op jit(solution)/shard_map/all_to_all | solution.py:94
  376.2 0.8 all_to_all.46
  377.0 4.9 %all-to-all-start.3 = ((bf16[8,4,4096]{2,1,0:T(4,128)(2,1)}), bf16[8,4,4096]{2,1,0:T(4,128)(2,1)S(1)}, u32[]{:S(2)}, u32[]{:S(2)}) async-start(bf16[8,4,4096]{2,1,0:T(4,128)(2,1)} %all_to_all.46), calls=%async_computation.3 | async-start | bytes 524288 | tf_op jit(solution)/shard_map/all_to_all | solution.py:97
  381.8 8.2 %fusion.17 = f32[1,224,4096]{2,1,0:T(8,128)} fusion(bf16[1024,224]{0,1:T(8,128)(2,1)S(1)} %copy-done.4, bf16[1024,8192]{1,0:T(8,128)(2,1)} %all-gather.4.cloned.1.call-done, f32[4096]{0:T(1024)S(1)} %bitcast.69, bf16[1,224,4096]{2,1,0:T(8,128)(2,1)} %param.20), kind=kOutput, calls=%fused_computation.11 | convolution fusion | flops 1886388224 | bytes 14368768 | tf_op jit(solution)/shard_map/dot_general | solution.py:89
  390.1 0.9 convolution_convert_fusion.2
  (33 shorter events, 2.8 us)
Async XLA Ops:
  7.2 160.7 %copy-start = (bf16[1,4096,224]{1,2,0:T(8,128)(2,1)S(1)}, bf16[1,4096,224]{1,2,0:T(8,128)(2,1)}, u32[]{:S(2)}) copy-start(bf16[1,4096,224]{1,2,0:T(8,128)(2,1)} %param.17) | copy-start | bytes 5505028
  7.2 160.6 %all-gather.4.cloned.1.call-start = ((), (), s32[]{:S(2)}) async-start(), calls=%async_computation.4 | async-start | bytes 17301504 | tf_op jit(solution)/shard_map/all_gather | solution.py:34
  28.2 306.4 %all-gather.6.cloned.1.call-start = ((), (), s32[]{:S(2)}) async-start(), calls=%async_computation.5 | async-start | bytes 15138816 | tf_op jit(solution)/shard_map/all_gather | solution.py:9
  167.8 8.2 %copy-start.6 = (bf16[1024,8192]{1,0:T(8,128)(2,1)S(1)}, bf16[1024,8192]{1,0:T(8,128)(2,1)}, u32[]{:S(2)}) copy-start(bf16[1024,8192]{1,0:T(8,128)(2,1)} %all-gather.4.cloned.1.call-done) | copy-start | bytes 50331652
  167.8 8.7 %copy-start.7 = (bf16[1,4096,224]{1,2,0:T(8,128)(2,1)S(1)}, bf16[1,4096,224]{1,2,0:T(8,128)(2,1)}, u32[]{:S(2)}) copy-start(bf16[1,4096,224]{1,2,0:T(8,128)(2,1)} %param.18) | copy-start | bytes 5505028
  176.5 3.6 copy-start.2
  180.5 1.5 copy-start.3
  182.9 0.7 copy-start.5
  186.5 164.7 %all-to-all-start.1 = ((bf16[224,32,128]{2,0,1:T(8,128)(2,1)}), bf16[224,32,128]{2,0,1:T(8,128)(2,1)S(1)}, u32[]{:S(2)}, u32[]{:S(2)}) async-start(bf16[224,32,128]{2,0,1:T(8,128)(2,1)} %copy.27), calls=%async_computation.1 | async-start | bytes 3670016 | tf_op jit(solution)/shard_map/all_to_all | solution.py:92
  351.2 30.6 %copy-start.4 = (bf16[1024,224]{0,1:T(8,128)(2,1)S(1)}, bf16[1024,224]{0,1:T(8,128)(2,1)}, u32[]{:S(2)}) copy-start(bf16[1024,224]{0,1:T(8,128)(2,1)} %fusion.32) | copy-start | bytes 1376260
  377.0 13.1 %all-to-all-start.3 = ((bf16[8,4,4096]{2,1,0:T(4,128)(2,1)}), bf16[8,4,4096]{2,1,0:T(4,128)(2,1)S(1)}, u32[]{:S(2)}, u32[]{:S(2)}) async-start(bf16[8,4,4096]{2,1,0:T(4,128)(2,1)} %all_to_all.46), calls=%async_computation.3 | async-start | bytes 524288 | tf_op jit(solution)/shard_map/all_to_all | solution.py:97
  381.8 9.2 %copy-start.1 = (bf16[1,4096,224]{1,2,0:T(8,128)(2,1)S(1)}, bf16[1,4096,224]{1,2,0:T(8,128)(2,1)}, u32[]{:S(2)}) copy-start(bf16[1,4096,224]{1,2,0:T(8,128)(2,1)} %param.17) | copy-start | bytes 5505028
Sparse Core Ops, SparseCore 0:
  28.3 139.4 all-gather.3
  180.2 154.3 all-gather.5
